TPU v7x, 32 devices: a whole 2x2x4 slice. The times are simulated.
32 devices in a mesh: grp: 4 (over y, x), zero: 8 (over z, core).
Axes of the slice: x: 2, y: 2, z: 4, core: 2. Of those that a mesh axis runs over, the one named last changes fastest.
Arguments:
- replica_grads: bfloat16 [4, 3072, 2, 12288], P('grp', None, None, 'zero'), may hold values from -20000 to 20000, as said below
- master_weights: float32 [3072, 2, 12288], P(('grp', 'zero')), may hold values from -0.6 to 0.6
- first_moment: float32 [3072, 2, 12288], P(('grp', 'zero')), may hold values from -0.3 to 0.3
- second_moment: float32 [3072, 2, 12288], P(('grp', 'zero')), may hold values from 0.001 to 0.03
- max_norm: float32 [1], replicated, may hold values from 1737.7856 to 4344.464
Outputs:
- new_master: float32 [3072, 2, 12288], P(('grp', 'zero'))
- new_first: float32 [3072, 2, 12288], P(('grp', 'zero'))
- new_second: float32 [3072, 2, 12288], P(('grp', 'zero'))
- new_weights: bfloat16 [3072, 2, 12288], P(None, None, 'zero')
Inputs may be any that keep to these rules, and one draw needn't show every extreme that they name: `replica_grads`: one gradient of the joined weight for each replica group.
All inputs are finite; a program needn't handle non-finite values.
Results may differ from a plain program's by a relative error of at most 0.015.
Values may be sent and summed in bfloat16 or wider, within the bound.
A program may use at most 192 MiB of HBM per device.

v0:
```python
import functools

import jax
import jax.numpy as jnp
from jax import lax
from jax.experimental import pallas as pl
from jax.experimental.pallas import tpu as pltpu
from jax.experimental.layout import Layout, with_layout_constraint
from jax.sharding import PartitionSpec as P

ADAM_STEP = 10
MESH = pl.DeviceIdType.MESH
LANES = 128

beta_one = 0.9
beta_two = 0.95
learn_rate = 0.02
adam_eps = 1e-08
norm_eps = 1e-06


def adam_update(summed, master, first, second, scale):
    clipped = summed * scale
    new_first = beta_one * first + (1.0 - beta_one) * clipped
    new_second = beta_two * second + (1.0 - beta_two) * clipped * clipped
    correct_one = 1.0 - beta_one**ADAM_STEP
    correct_two = 1.0 - beta_two**ADAM_STEP
    step_size = new_first / correct_one / (jnp.sqrt(new_second / correct_two) + adam_eps)
    new_master = master - learn_rate * step_size
    return (new_master, new_first, new_second)


def plain_body(replica_grads, master_weights, first_moment, second_moment, max_norm):
    groups = lax.axis_size("grp")
    shards = lax.axis_size("zero")
    local_grad = replica_grads[0]
    local_width = local_grad.shape[2]
    rows_dev = master_weights.shape[0]
    full_width = master_weights.shape[2]
    blocks = local_grad.reshape(groups, shards, rows_dev, 2, local_width)
    arrived = lax.all_to_all(
        lax.all_to_all(blocks[None], "grp", split_axis=1, concat_axis=0, tiled=True),
        "zero",
        split_axis=2,
        concat_axis=5,
        tiled=True,
    )
    summed = jnp.sum(arrived.astype(jnp.float32), axis=0)
    summed = summed.reshape(master_weights.shape)
    total = lax.psum(jnp.sum(summed * summed), ("grp", "zero"))
    scale = jnp.minimum(jnp.float32(1.0), max_norm[0] / (jnp.sqrt(total) + norm_eps))
    new_master, new_first, new_second = adam_update(
        summed, master_weights, first_moment, second_moment, scale
    )
    fresh = new_master.astype(jnp.bfloat16).reshape(1, 1, rows_dev, 2, full_width)
    own_tiles = lax.all_to_all(fresh, "zero", split_axis=4, concat_axis=1, tiled=True)
    tiled = lax.all_gather(own_tiles, "grp", axis=0, tiled=True)
    new_weights = tiled.reshape(groups * shards * rows_dev, 2, full_width // shards)
    return (new_master, new_first, new_second, new_weights)


def flip(index, mask, size):
    out = 0
    bit = 1
    while bit < size:
        b = (index // bit) % 2
        out = out + bit * ((1 - b) if mask & bit else b)
        bit *= 2
    return out


def greet(groups, shards, g, z):
    barrier = pltpu.get_barrier_semaphore()
    for k in range(1, shards):
        pl.semaphore_signal(barrier, inc=1, device_id=(g, flip(z, k, shards)), device_id_type=MESH)
    for j in range(1, groups):
        pl.semaphore_signal(barrier, inc=1, device_id=(flip(g, j, groups), z), device_id_type=MESH)
    pl.semaphore_wait(barrier, shards + groups - 2)


def remote(src, dst, send, recv, device):
    return pltpu.make_async_remote_copy(
        src_ref=src, dst_ref=dst, send_sem=send, recv_sem=recv,
        device_id=device, device_id_type=MESH,
    )


def scatter_kernel(groups, shards, grad, landed, norm, near, far, own, kept, pairs, got, sums, zone, gone,
                   f_send, f_recv, load_sem, p_send, p_recv, s_send, s_recv,
                   nz_send, nz_recv, ng_send, ng_recv, loc_sem):
    g, z = lax.axis_index("grp"), lax.axis_index("zero")
    gx, gy, diagonal = flip(g, 1, groups), flip(g, 2, groups), flip(g, 3, groups)
    first_to, second_to = (gx, gy), (gy, gx)
    rows = own.shape[2]
    order = list(range(shards - 1, -1, -1))

    def raw(k, h, d):
        block = diagonal if d else first_to[h]
        return remote(grad.at[block, flip(z, k, shards), h], (far if d else near).at[k, h],
                      f_send.at[k, h, d], f_recv.at[k, h, d], (first_to[h], z))

    def pair(k, h):
        return remote(pairs.at[k, h], got.at[k, h], p_send.at[k, h], p_recv.at[k, h], (second_to[h], z))

    def load(k, h, d):
        block = second_to[h] if d else g
        return pltpu.make_async_copy(grad.at[block, flip(z, k, shards), h], (kept if d else own).at[k, h],
                                     load_sem.at[k, h, d])

    def onward(k):
        return remote(sums.at[k], landed.at[z], s_send.at[k], s_recv.at[k], (g, flip(z, k, shards)))

    def begin(k):
        for d in (1, 0):
            for h in (0, 1):
                raw(k, h, d).start()

    for k in order:
        for d in (1, 0):
            for h in (0, 1):
                load(k, h, d).start()
    greet(groups, shards, g, z)
    ahead = 3
    for k in order[:ahead]:
        begin(k)
    stay = pltpu.make_async_copy(sums.at[0], landed.at[z], loc_sem)
    square = jnp.zeros(own.shape[3:], jnp.float32)
    for i in range(shards + 1):
        if i < shards:
            k = order[i]
            for h in (0, 1):
                load(k, h, 1).wait()
                raw(k, h, 1).wait_recv()

                def join(r, carry, k=k, h=h):
                    both = kept[k, h, r].astype(jnp.float32) + far[k, h, r].astype(jnp.float32)
                    pairs[k, h, r] = both.astype(jnp.bfloat16)
                    return carry

                lax.fori_loop(0, rows, join, 0)
                pair(k, h).start()
            if i + ahead < shards:
                begin(order[i + ahead])
        if i >= 1:
            k = order[i - 1]
            for h in (0, 1):
                load(k, h, 0).wait()
                raw(k, h, 0).wait_recv()
                pair(k, h).wait_recv()

                def add(r, acc, k=k, h=h):
                    total = own[k, h, r].astype(jnp.float32) + near[k, h, r].astype(jnp.float32)
                    total = total + got[k, h, r].astype(jnp.float32)
                    sums[k, h, r] = total.astype(jnp.bfloat16)
                    return acc + total * total

                square = lax.fori_loop(0, rows, add, square)
            if k:
                onward(k).start()
            else:
                stay.start()

    folded = square[0:8]
    for i in range(8, square.shape[0], 8):
        folded = folded + square[i:i + 8]
    zone[0] = folded

    def tell_zero(k):
        return remote(zone.at[0], zone.at[k], nz_send.at[k], nz_recv.at[k], (g, flip(z, k, shards)))

    def tell_group(j):
        return remote(gone.at[0], gone.at[j], ng_send.at[j], ng_recv.at[j], (flip(g, j, groups), z))

    for k in range(1, shards):
        tell_zero(k).start()
    for k in range(1, shards):
        tell_zero(k).wait_recv()
    gone[0] = jnp.sum(zone[...], axis=0)
    for j in range(1, groups):
        tell_group(j).start()
    for j in range(1, groups):
        tell_group(j).wait_recv()
    norm[...] = jnp.sum(gone[...], axis=0)

    for k in range(1, shards):
        tell_zero(k).wait_send()
    for j in range(1, groups):
        tell_group(j).wait_send()
    for k in order:
        for h in (0, 1):
            pair(k, h).wait_send()
            for d in (0, 1):
                raw(k, h, d).wait_send()
        if k:
            onward(k).wait()
        else:
            stay.wait()


def update_kernel(limit, norm, summed, master, first, second, out_master, out_first, out_second, fresh):
    total = jnp.full(master.shape[2:], jnp.sum(norm[...]), jnp.float32)
    scale = jnp.minimum(jnp.float32(1.0), limit[0] / (jnp.sqrt(total) + norm_eps))

    rate_one = learn_rate / (1.0 - beta_one**ADAM_STEP)
    over_two = 1.0 / (1.0 - beta_two**ADAM_STEP)

    def row(r, carry):
        for c in range(summed.shape[0]):
            clipped = summed[c, r].astype(jnp.float32) * scale
            new_first = beta_one * first[r, c] + (1.0 - beta_one) * clipped
            new_second = beta_two * second[r, c] + (1.0 - beta_two) * clipped * clipped
            below = jnp.sqrt(new_second * over_two) + adam_eps
            new_master = master[r, c] - new_first * rate_one / below
            out_master[r, c] = new_master
            out_first[r, c] = new_first
            out_second[r, c] = new_second
            fresh[c, r] = new_master.astype(jnp.bfloat16)
        return carry

    lax.fori_loop(0, master.shape[0], row, 0)


def gather_kernel(groups, shards, fresh, out, hold, z_send, z_recv, x_send, x_recv, y_send, y_recv,
                  u_send, u_recv, v_send, v_recv, loc_sem):
    g, z = lax.axis_index("grp"), lax.axis_index("zero")
    half = fresh.shape[1] // 2
    gx, gy = flip(g, 1, groups), flip(g, 2, groups)

    def spread(k):
        return remote(fresh.at[flip(z, k, shards)], out.at[g, z], z_send.at[k], z_recv.at[k],
                      (g, flip(z, k, shards)))

    def first_hop(k, send, recv, to):
        q = flip(z, k, shards)
        src = out.at[g, q] if k else fresh.at[z]
        return remote(src, out.at[g, q], send.at[k], recv.at[k], (to, z))

    def second_hop(k, origin, start, send, recv, to):
        q = flip(z, k, shards)
        ref = out.at[origin, q, pl.ds(start, half)]
        return remote(ref, ref, send.at[k], recv.at[k], (to, z))

    def hops(k):
        return (first_hop(k, x_send, x_recv, gx), first_hop(k, y_send, y_recv, gy))

    def turns(k):
        return (second_hop(k, gx, 0, u_send, u_recv, gy), second_hop(k, gy, half, v_send, v_recv, gx))

    load = pltpu.make_async_copy(fresh.at[z], hold, loc_sem.at[0])
    store = pltpu.make_async_copy(hold, out.at[g, z], loc_sem.at[1])
    load.start()
    greet(groups, shards, g, z)
    for k in range(1, shards):
        spread(k).start()
    lag = 1
    for s in range(shards + lag):
        if s < shards:
            if s:
                spread(s).wait_recv()
            for hop in hops(s):
                hop.start()
            if s == 0:
                load.wait()
                store.start()
        if s >= lag:
            for hop, turn in zip(hops(s - lag), turns(s - lag)):
                hop.wait_recv()
                turn.start()
    store.wait()
    for k in range(shards):
        if k:
            spread(k).wait_send()
        for hop in hops(k):
            hop.wait_send()
        for turn in turns(k):
            turn.wait()


def flat_body(replica_grads, master_weights, first_moment, second_moment, max_norm):
    groups = lax.axis_size("grp")
    shards = lax.axis_size("zero")
    rows = master_weights.shape[0]
    width = replica_grads.shape[3]
    tiles = width // LANES
    deep = 2 * tiles
    bf16, f32 = jnp.bfloat16, jnp.float32
    any_space = pl.BlockSpec(memory_space=pl.ANY)
    dma = pltpu.SemaphoreType.DMA
    limit = 60 * 1024 * 1024

    def keep(x, *order):
        return with_layout_constraint(x, Layout(major_to_minor=order))

    def flat(x):
        x = x.reshape(x.shape[0], 2, -1, LANES)
        return jnp.swapaxes(keep(x, 0, 2, 1, 3), 1, 2)

    grad = flat(replica_grads[0]).reshape(groups, shards, 2, rows // 2, deep, LANES)
    master, first, second = (
        flat(x).reshape(rows, shards, deep, LANES)
        for x in (master_weights, first_moment, second_moment)
    )

    piece = (rows, deep, LANES)
    halves = (shards, 2, rows // 2, deep, LANES)
    landed, norm = pl.pallas_call(
        functools.partial(scatter_kernel, groups, shards),
        out_shape=(
            jax.ShapeDtypeStruct(halves, bf16),
            jax.ShapeDtypeStruct((8, LANES), f32),
        ),
        in_specs=[any_space],
        out_specs=(any_space, pl.BlockSpec(memory_space=pltpu.VMEM)),
        scratch_shapes=[
            *[pltpu.VMEM(halves, bf16)] * 7,
            pltpu.VMEM((shards, 8, LANES), f32),
            pltpu.VMEM((groups, 8, LANES), f32),
            *[dma((shards, 2, 2))] * 3,
            *[dma((shards, 2))] * 2,
            *[dma((shards,))] * 4,
            dma((groups,)),
            dma((groups,)),
            dma,
        ],
        compiler_params=pltpu.CompilerParams(
            collective_id=0, has_side_effects=True, vmem_limit_bytes=limit
        ),
    )(grad)

    step = 8 if rows % 8 == 0 else 1
    by_row = pl.BlockSpec((step, shards, deep, LANES), lambda i: (i, 0, 0, 0))
    by_shard = pl.BlockSpec((shards, step, deep, LANES), lambda i: (0, i, 0, 0))
    state = jax.ShapeDtypeStruct((rows, shards, deep, LANES), f32)
    new_master, new_first, new_second, fresh = pl.pallas_call(
        update_kernel,
        grid=(rows // step,),
        out_shape=(state, state, state, jax.ShapeDtypeStruct((shards,) + piece, bf16)),
        in_specs=[
            pl.BlockSpec(memory_space=pltpu.SMEM),
            pl.BlockSpec((8, LANES), lambda i: (0, 0)),
            by_shard, by_row, by_row, by_row,
        ],
        out_specs=(by_row, by_row, by_row, by_shard),
        compiler_params=pltpu.CompilerParams(vmem_limit_bytes=limit),
    )(max_norm, norm, landed.reshape((shards,) + piece), master, first, second)

    gathered = pl.pallas_call(
        functools.partial(gather_kernel, groups, shards),
        out_shape=jax.ShapeDtypeStruct((groups, shards) + piece, bf16),
        in_specs=[any_space],
        out_specs=any_space,
        scratch_shapes=[pltpu.VMEM(piece, bf16)] + [dma((shards,))] * 10 + [dma((2,))],
        compiler_params=pltpu.CompilerParams(
            collective_id=1, has_side_effects=True, vmem_limit_bytes=limit
        ),
    )(fresh)

    def unflat(x, shape):
        x = x.reshape(shape[0], -1, 2, LANES)
        return keep(jnp.swapaxes(x, 1, 2), 0, 2, 1, 3).reshape(shape)

    shape = master_weights.shape
    return (
        unflat(new_master, shape),
        unflat(new_first, shape),
        unflat(new_second, shape),
        unflat(gathered, replica_grads.shape[1:]),
    )


def body(replica_grads, master_weights, first_moment, second_moment, max_norm):
    groups = lax.axis_size("grp")
    shards = lax.axis_size("zero")
    rows = master_weights.shape[0]
    width = replica_grads.shape[3]
    deep = 2 * width // LANES
    power = shards > 1 and shards & (shards - 1) == 0
    fits = groups * shards * rows * deep * LANES * 2 * 7 // 4 < 48 * 1024 * 1024
    whole = width % LANES == 0 and deep % 8 == 0 and rows % 2 == 0
    run = flat_body if groups == 4 and power and fits and whole else plain_body
    return run(replica_grads, master_weights, first_moment, second_moment, max_norm)


def solution(mesh):
    in_specs = (
        P("grp", None, None, "zero"),
        P(("grp", "zero"), None, None),
        P(("grp", "zero"), None, None),
        P(("grp", "zero"), None, None),
        P(),
    )
    out_specs = (
        P(("grp", "zero"), None, None),
        P(("grp", "zero"), None, None),
        P(("grp", "zero"), None, None),
        P(None, None, "zero"),
    )
    return jax.shard_map(body, mesh=mesh, in_specs=in_specs, out_specs=out_specs, check_vma=False)
```

profile of v0, /device:TPU:0, one launch (start us, length us, event | category | flops | bytes accessed | tf_op | source)
XLA Modules:
  0.0 395.3 jit_solution(2341277688619584491)
XLA Ops:
  1.3 186.1 %shard_map.84 = (bf16[8,2,48,24,128]{4,3,2,1,0:T(8,128)(2,1)}, f32[8,128]{1,0:T(8,128)}) custom-call(bf16[4,8,2,48,24,128]{5,4,3,2,1,0:T(8,128)(2,1)} %bitcast.42), custom_call_target="tpu_custom_call" | custom-call | tf_op jit(solution)/shard_map/pallas_call | solution.py:306
  187.3 27.7 %shard_map.85 = (f32[96,8,24,128]{3,2,1,0:T(8,128)}, f32[96,8,24,128]{3,2,1,0:T(8,128)}, f32[96,8,24,128]{3,2,1,0:T(8,128)}, bf16[8,96,24,128]{3,2,1,0:T(8,128)(2,1)}) custom-call(f32[1]{0:T(128)S(6)} %copy.10.limit, f32[8,128]{1,0:T(8,128)} %get-tuple-element.10.norm, bf16[8,96,24,128]{3,2,1,0:T(8,128)(2,1)} %bitcast.46, f32[96,8,24,128]{3,2,1,0:T(8,128)} %bitcast.43, ...), custom_call_target="tpu_custom_call" | custom-call | tf_op jit(solution)/shard_map/pallas_call | solution.py:334
  215.0 164.4 %shard_map.86 = bf16[4,8,96,24,128]{4,3,2,1,0:T(8,128)(2,1)} custom-call(bf16[8,96,24,128]{3,2,1,0:T(8,128)(2,1)} %get-tuple-element.15.fresh), custom_call_target="tpu_custom_call" | custom-call | tf_op jit(solution)/shard_map/pallas_call | solution.py:347
  379.5 15.8 %copy.11 = bf16[3072,2,1536]{2,1,0:T(2,128)(2,1)} copy(bf16[3072,2,1536]{2,1,0:T(2,128)(2,1)} %bitcast.41) | data formatting | bytes 37748736
where the time goes:
time: 396 us; the launch traced here: 395 us
  Pallas kernels  378 us (95%)
  local copies, waits for them, and re-layouts  15.8 us (4%)
    pallas_call x1, Pallas kernels, flat_body(): pl.pallas_call(functools.partial(scatter_kernel, groups, shards), out_sha...  186 us
    pallas_call x1, Pallas kernels, flat_body(): pl.pallas_call(functools.partial(gather_kernel, groups, shards), out_shap...  164 us
    pallas_call x1, Pallas kernels, flat_body(): pl.pallas_call(update_kernel, grid=(rows // step,), out_shape=(state, sta...  27.7 us
    unnamed x1, local copies, waits for them, and re-layouts  15.8 us

commit v1 on v0

v1 whole, which is shorter than its diff:
```python
import functools

import jax
import jax.numpy as jnp
from jax import lax
from jax.experimental import pallas as pl
from jax.experimental.pallas import tpu as pltpu
from jax.experimental.layout import Layout, with_layout_constraint
from jax.sharding import PartitionSpec as P

ADAM_STEP = 10
MESH = pl.DeviceIdType.MESH
LANES = 128

beta_one = 0.9
beta_two = 0.95
learn_rate = 0.02
adam_eps = 1e-08
norm_eps = 1e-06


def adam_update(summed, master, first, second, scale):
    clipped = summed * scale
    new_first = beta_one * first + (1.0 - beta_one) * clipped
    new_second = beta_two * second + (1.0 - beta_two) * clipped * clipped
    correct_one = 1.0 - beta_one**ADAM_STEP
    correct_two = 1.0 - beta_two**ADAM_STEP
    step_size = new_first / correct_one / (jnp.sqrt(new_second / correct_two) + adam_eps)
    new_master = master - learn_rate * step_size
    return (new_master, new_first, new_second)


def plain_body(replica_grads, master_weights, first_moment, second_moment, max_norm):
    groups = lax.axis_size("grp")
    shards = lax.axis_size("zero")
    local_grad = replica_grads[0]
    local_width = local_grad.shape[2]
    rows_dev = master_weights.shape[0]
    full_width = master_weights.shape[2]
    blocks = local_grad.reshape(groups, shards, rows_dev, 2, local_width)
    arrived = lax.all_to_all(
        lax.all_to_all(blocks[None], "grp", split_axis=1, concat_axis=0, tiled=True),
        "zero",
        split_axis=2,
        concat_axis=5,
        tiled=True,
    )
    summed = jnp.sum(arrived.astype(jnp.float32), axis=0)
    summed = summed.reshape(master_weights.shape)
    total = lax.psum(jnp.sum(summed * summed), ("grp", "zero"))
    scale = jnp.minimum(jnp.float32(1.0), max_norm[0] / (jnp.sqrt(total) + norm_eps))
    new_master, new_first, new_second = adam_update(
        summed, master_weights, first_moment, second_moment, scale
    )
    fresh = new_master.astype(jnp.bfloat16).reshape(1, 1, rows_dev, 2, full_width)
    own_tiles = lax.all_to_all(fresh, "zero", split_axis=4, concat_axis=1, tiled=True)
    tiled = lax.all_gather(own_tiles, "grp", axis=0, tiled=True)
    new_weights = tiled.reshape(groups * shards * rows_dev, 2, full_width // shards)
    return (new_master, new_first, new_second, new_weights)


def flip(index, mask, size):
    out = 0
    bit = 1
    while bit < size:
        b = (index // bit) % 2
        out = out + bit * ((1 - b) if mask & bit else b)
        bit *= 2
    return out


def greet(groups, shards, g, z):
    barrier = pltpu.get_barrier_semaphore()
    for k in range(1, shards):
        pl.semaphore_signal(barrier, inc=1, device_id=(g, flip(z, k, shards)), device_id_type=MESH)
    for j in range(1, groups):
        pl.semaphore_signal(barrier, inc=1, device_id=(flip(g, j, groups), z), device_id_type=MESH)
    pl.semaphore_wait(barrier, shards + groups - 2)


def remote(src, dst, send, recv, device):
    return pltpu.make_async_remote_copy(
        src_ref=src, dst_ref=dst, send_sem=send, recv_sem=recv,
        device_id=device, device_id_type=MESH,
    )


def step_kernel(groups, shards, limit, grad, master_in, first_in, second_in, master, first, second, out,
                sums, landed, zone, gone, f_send, f_recv, load_sem, p_send, p_recv, s_send, s_recv,
                nz_send, nz_recv, ng_send, ng_recv, state_sem, z_send, z_recv, x_send, x_recv, y_send, y_recv,
                u_send, u_recv, v_send, v_recv):
    g, z = lax.axis_index("grp"), lax.axis_index("zero")
    gx, gy, diagonal = flip(g, 1, groups), flip(g, 2, groups), flip(g, 3, groups)
    first_to, second_to = (gx, gy), (gy, gx)
    rows = landed.shape[1]
    half = rows // 2
    order = list(range(shards - 1, -1, -1))
    near, far, got, pairs = (out.at[i] for i in range(4))
    bf16, f32 = jnp.bfloat16, jnp.float32

    def part(ref, k, h):
        return ref.at[k, pl.ds(h * half, half)]

    def raw(k, h, d):
        block = diagonal if d else first_to[h]
        return remote(grad.at[block, flip(z, k, shards), h], part(far if d else near, k, h),
                      f_send.at[k, h, d], f_recv.at[k, h, d], (first_to[h], z))

    def pair(k, h):
        return remote(part(pairs, k, h), part(got, k, h), p_send.at[k, h], p_recv.at[k, h], (second_to[h], z))

    def load(k, h, d):
        block = second_to[h] if d else g
        return pltpu.make_async_copy(grad.at[block, flip(z, k, shards), h], part(pairs if d else sums, k, h),
                                     load_sem.at[k, h, d])

    def onward(k):
        return remote(sums.at[k], landed.at[z], s_send.at[k], s_recv.at[k], (g, flip(z, k, shards)))

    states = [
        pltpu.make_async_copy(src, dst, state_sem.at[i])
        for i, (src, dst) in enumerate(((master_in, master), (first_in, first), (second_in, second)))
    ]

    greet(groups, shards, g, z)
    ahead = 2
    for k in order[:ahead]:
        for h in (0, 1):
            raw(k, h, 1).start()
    for k in order:
        for d in (1, 0):
            for h in (0, 1):
                load(k, h, d).start()
    for state in states:
        state.start()
    square = jnp.zeros(landed.shape[2:], f32)
    for i in range(shards + 1):
        if i < shards:
            k = order[i]
            for h in (0, 1):
                load(k, h, 1).wait()
                raw(k, h, 1).wait_recv()

                def join(r, carry, k=k, h=h):
                    row = h * half + r
                    both = pairs[k, row].astype(f32) + far[k, row].astype(f32)
                    pairs[k, row] = both.astype(bf16)
                    return carry

                lax.fori_loop(0, half, join, 0)
                pair(k, h).start()
            for h in (0, 1):
                raw(k, h, 0).start()
            if i + ahead < shards:
                for h in (0, 1):
                    raw(order[i + ahead], h, 1).start()
        if i >= 1:
            k = order[i - 1]
            for h in (0, 1):
                load(k, h, 0).wait()
                raw(k, h, 0).wait_recv()
                pair(k, h).wait_recv()

                def add(r, acc, k=k, h=h):
                    row = h * half + r
                    total = sums[k, row].astype(f32) + near[k, row].astype(f32)
                    total = total + got[k, row].astype(f32)
                    if k:
                        sums[k, row] = total.astype(bf16)
                    else:
                        landed[z, row] = total.astype(bf16)
                    return acc + total * total

                square = lax.fori_loop(0, half, add, square)
            if k:
                onward(k).start()

    folded = square[0:8]
    for i in range(8, square.shape[0], 8):
        folded = folded + square[i:i + 8]
    zone[0] = folded

    def tell_zero(k):
        return remote(zone.at[0], zone.at[k], nz_send.at[k], nz_recv.at[k], (g, flip(z, k, shards)))

    def tell_group(j):
        return remote(gone.at[0], gone.at[j], ng_send.at[j], ng_recv.at[j], (flip(g, j, groups), z))

    for k in order:
        for h in (0, 1):
            pair(k, h).wait_send()
    for k in range(1, shards):
        tell_zero(k).start()
    for k in range(1, shards):
        tell_zero(k).wait_recv()
    gone[0] = jnp.sum(zone[...], axis=0)
    for j in range(1, groups):
        tell_group(j).start()
    for j in range(1, groups):
        tell_group(j).wait_recv()
    norm = jnp.sum(gone[...], axis=0)
    total = jnp.full(landed.shape[2:], jnp.sum(norm), f32)
    scale = jnp.minimum(f32(1.0), limit[0] / (jnp.sqrt(total) + norm_eps))
    rate_one = learn_rate / (1.0 - beta_one**ADAM_STEP)
    over_two = 1.0 / (1.0 - beta_two**ADAM_STEP)

    def update(k):
        c = flip(z, k, shards)

        def row(r, carry):
            clipped = landed[c, r].astype(f32) * scale
            new_first = beta_one * first[r, c] + (1.0 - beta_one) * clipped
            new_second = beta_two * second[r, c] + (1.0 - beta_two) * clipped * clipped
            below = jnp.sqrt(new_second * over_two) + adam_eps
            new_master = master[r, c] - new_first * rate_one / below
            master[r, c] = new_master
            first[r, c] = new_first
            second[r, c] = new_second
            if k:
                landed[c, r] = new_master.astype(bf16)
            else:
                out[g, z, r] = new_master.astype(bf16)
            return carry

        lax.fori_loop(0, rows, row, 0)

    def spread(k):
        return remote(landed.at[flip(z, k, shards)], out.at[g, z], z_send.at[k], z_recv.at[k],
                      (g, flip(z, k, shards)))

    def first_hop(k, send, recv, to):
        ref = out.at[g, flip(z, k, shards)]
        return remote(ref, ref, send.at[k], recv.at[k], (to, z))

    def second_hop(k, origin, start, send, recv, to):
        ref = out.at[origin, flip(z, k, shards), pl.ds(start, half)]
        return remote(ref, ref, send.at[k], recv.at[k], (to, z))

    def hops(k):
        return (first_hop(k, x_send, x_recv, gx), first_hop(k, y_send, y_recv, gy))

    def turns(k):
        return (second_hop(k, gx, 0, u_send, u_recv, gy), second_hop(k, gy, half, v_send, v_recv, gx))

    for state in states:
        state.wait()
    update(0)
    for hop in hops(0):
        hop.start()
    for k in range(1, shards):
        onward(k).wait_recv()
        update(k)
        spread(k).start()
    lag = 1
    for s in range(1, shards + lag):
        if s < shards:
            spread(s).wait_recv()
            for hop in hops(s):
                hop.start()
        if s >= lag:
            for hop, turn in zip(hops(s - lag), turns(s - lag)):
                hop.wait_recv()
                turn.start()
    for k in range(1, shards):
        tell_zero(k).wait_send()
        onward(k).wait_send()
        spread(k).wait_send()
    for j in range(1, groups):
        tell_group(j).wait_send()
    for k in order:
        for h in (0, 1):
            for d in (0, 1):
                raw(k, h, d).wait_send()
        for hop in hops(k):
            hop.wait_send()
        for turn in turns(k):
            turn.wait()


def store_kernel(pieces, *refs):
    count = len(refs) // 2
    sources, targets, sem = refs[:count], refs[count:2 * count], refs[-1]
    copies = []
    for i, (source, target) in enumerate(zip(sources, targets)):
        size = source.shape[0] // pieces
        for j in range(pieces):
            span = pl.ds(j * size, size)
            copies.append(pltpu.make_async_copy(source.at[span], target.at[span], sem.at[i, j]))
    for copy in copies:
        copy.start()
    for copy in copies:
        copy.wait()


def flat_body(replica_grads, master_weights, first_moment, second_moment, max_norm):
    groups = lax.axis_size("grp")
    shards = lax.axis_size("zero")
    rows = master_weights.shape[0]
    width = replica_grads.shape[3]
    tiles = width // LANES
    deep = 2 * tiles
    bf16, f32 = jnp.bfloat16, jnp.float32
    any_space = pl.BlockSpec(memory_space=pl.ANY)
    vmem = pl.BlockSpec(memory_space=pltpu.VMEM)
    dma = pltpu.SemaphoreType.DMA

    def keep(x, *order):
        return with_layout_constraint(x, Layout(major_to_minor=order))

    def flat(x):
        x = x.reshape(x.shape[0], 2, -1, LANES)
        return jnp.swapaxes(keep(x, 0, 2, 1, 3), 1, 2)

    grad = flat(replica_grads[0]).reshape(groups, shards, 2, rows // 2, deep, LANES)
    master, first, second = (
        flat(x).reshape(rows, shards, deep, LANES)
        for x in (master_weights, first_moment, second_moment)
    )

    block = (shards, rows, deep, LANES)
    state = (rows, shards, deep, LANES)
    grant = 4 * shards * rows * deep * LANES + 192 * 1024
    results = pl.pallas_call(
        functools.partial(step_kernel, groups, shards),
        out_shape=(*[pltpu.VMEM(state, f32)] * 3, pltpu.VMEM((groups,) + block, bf16)),
        in_specs=[pl.BlockSpec(memory_space=pltpu.SMEM)] + [any_space] * 4,
        out_specs=(vmem,) * 4,
        scratch_shapes=[
            *[pltpu.VMEM(block, bf16)] * 2,
            pltpu.VMEM((shards, 8, LANES), f32),
            pltpu.VMEM((groups, 8, LANES), f32),
            *[dma((shards, 2, 2))] * 3,
            *[dma((shards, 2))] * 2,
            *[dma((shards,))] * 4,
            *[dma((groups,))] * 2,
            dma((3,)),
            *[dma((shards,))] * 10,
        ],
        compiler_params=pltpu.CompilerParams(
            collective_id=0, has_side_effects=True, vmem_limit_bytes=grant
        ),
    )(max_norm, grad, master, first, second)

    pieces = 4
    *states, gathered = results
    new_master, new_first, new_second = pl.pallas_call(
        functools.partial(store_kernel, pieces),
        out_shape=(
            *[jax.ShapeDtypeStruct(state, f32)] * 3,
        ),
        in_specs=[any_space] * 3,
        out_specs=(any_space,) * 3,
        scratch_shapes=[dma((3, pieces))],
        compiler_params=pltpu.CompilerParams(vmem_limit_bytes=grant),
    )(*states)

    def unflat(x, shape):
        x = x.reshape(shape[0], -1, 2, LANES)
        return keep(jnp.swapaxes(x, 1, 2), 0, 2, 1, 3).reshape(shape)

    shape = master_weights.shape
    return (
        unflat(new_master, shape),
        unflat(new_first, shape),
        unflat(new_second, shape),
        unflat(gathered, replica_grads.shape[1:]),
    )


def body(replica_grads, master_weights, first_moment, second_moment, max_norm):
    groups = lax.axis_size("grp")
    shards = lax.axis_size("zero")
    rows = master_weights.shape[0]
    width = replica_grads.shape[3]
    deep = 2 * width // LANES
    power = shards > 1 and shards & (shards - 1) == 0
    fits = shards * rows * deep * LANES * (2 * groups + 12 + 4) < 63 * 1024 * 1024
    whole = width % LANES == 0 and deep % 8 == 0 and rows % 2 == 0
    run = flat_body if groups == 4 and power and fits and whole else plain_body
    return run(replica_grads, master_weights, first_moment, second_moment, max_norm)


def solution(mesh):
    in_specs = (
        P("grp", None, None, "zero"),
        P(("grp", "zero"), None, None),
        P(("grp", "zero"), None, None),
        P(("grp", "zero"), None, None),
        P(),
    )
    out_specs = (
        P(("grp", "zero"), None, None),
        P(("grp", "zero"), None, None),
        P(("grp", "zero"), None, None),
        P(None, None, "zero"),
    )
    return jax.shard_map(body, mesh=mesh, in_specs=in_specs, out_specs=out_specs, check_vma=False)
```

time: 396 us -> 350 us (0.88)
  Pallas kernels: 378 us -> 342 us
  local copies, waits for them, and re-layouts: 15.8 us -> 6.85 us
    pallas_call x3 -> x2, Pallas kernels: 378 us -> 342 us  [the longest x1 332 us: flat_body(): pl.pallas_call(functools.partial(step_kernel, groups, shards), out_shape=...]
    unnamed x1, local copies, waits for them, and re-layouts: 15.8 us -> 6.85 us
where the time goes in v1:
time: 350 us
  Pallas kernels  342 us (98%)
  local copies, waits for them, and re-layouts  6.85 us (2%)
    pallas_call x1, Pallas kernels, flat_body(): pl.pallas_call(functools.partial(step_kernel, groups, shards), out_shape=...  332 us
    pallas_call x1, Pallas kernels, flat_body(): pl.pallas_call(functools.partial(store_kernel, pieces), out_shape=(*[jax....  9.45 us

profile of v1, /device:TPU:0, one launch (start us, length us, event | category | flops | bytes accessed | tf_op | source)
XLA Modules:
  0.0 349.9 jit_solution(15838851363162455639)
XLA Ops:
  1.3 332.3 %shard_map.84 = (f32[96,8,24,128]{3,2,1,0:T(8,128)S(1)}, f32[96,8,24,128]{3,2,1,0:T(8,128)S(1)}, f32[96,8,24,128]{3,2,1,0:T(8,128)S(1)}, bf16[4,8,96,24,128]{4,3,2,1,0:T(8,128)(2,1)S(1)}) custom-call(f32[1]{0:T(128)S(6)} %copy.11.limit, bf16[4,8,2,48,24,128]{5,4,3,2,1,0:T(8,128)(2,1)} %bitcast.41, f32[96,8,24,128]{3,2,1,0:T(8,128)} %bitcast.42, ...), custom_call_target="tpu_custom_call" | custom-call | tf_op jit(solution)/shard_map/pallas_call | solution.py:323
  333.6 9.5 %shard_map.85 = (f32[96,8,24,128]{3,2,1,0:T(8,128)}, f32[96,8,24,128]{3,2,1,0:T(8,128)}, f32[96,8,24,128]{3,2,1,0:T(8,128)}) custom-call(f32[96,8,24,128]{3,2,1,0:T(8,128)S(1)} %get-tuple-element.11.refs_0_, f32[96,8,24,128]{3,2,1,0:T(8,128)S(1)} %get-tuple-element.12.refs_1_, f32[96,8,24,128]{3,2,1,0:T(8,128)S(1)} %get-tuple-element.13.refs_2_), custom_call_target="tpu_custom_call" | custom-call | tf_op jit(solution)/shard_map/pallas_call | solution.py:346
  343.0 6.9 %copy.10 = bf16[3072,2,1536]{2,1,0:T(2,128)(2,1)} copy(bf16[3072,2,1536]{2,1,0:T(2,128)(2,1)S(1)} %bitcast.40) | data formatting | bytes 37748736

commit v2 on v1

--- a/solution.py
+++ b/solution.py
@@ -85,8 +85,28 @@
     )
 
 
-def step_kernel(groups, shards, limit, grad, master_in, first_in, second_in, master, first, second, out,
-                sums, landed, zone, gone, f_send, f_recv, load_sem, p_send, p_recv, s_send, s_recv,
+def orders(shards):
+    used = [k for k in range(shards) if k != 3 or shards == 4]
+    used += [3] * (shards > 4)
+    made = [k for k in (shards // 2, 2, shards // 2 + 2, 1) if 0 < k < shards]
+    made = list(dict.fromkeys(made + used[1:]))
+    return used, made
+
+
+def partner(z, k, shards):
+    low, high = shards // 4, shards // 2
+    if low < 2 or k < high:
+        return k, flip(z, k, shards)
+    one, two = (z // low) % 2, (z // high) % 2
+    end = 1 - one - two + 2 * one * two
+    return (
+        k + end * ((k ^ low) - k),
+        flip(z, k, shards) * (1 - end) + flip(z, k ^ low, shards) * end,
+    )
+
+
+def step_kernel(groups, shards, tails, limit, grad, master_in, first_in, second_in, master, first, second, out,
+                late_x, late_y, sums, landed, zone, gone, f_send, f_recv, load_sem, p_send, p_recv, s_send, s_recv,
                 nz_send, nz_recv, ng_send, ng_recv, state_sem, z_send, z_recv, x_send, x_recv, y_send, y_recv,
                 u_send, u_recv, v_send, v_recv):
     g, z = lax.axis_index("grp"), lax.axis_index("zero")
@@ -95,6 +115,8 @@
     rows = landed.shape[1]
     half = rows // 2
     order = list(range(shards - 1, -1, -1))
+    used, made = orders(shards)
+    late = used[shards - tails:]
     near, far, got, pairs = (out.at[i] for i in range(4))
     bf16, f32 = jnp.bfloat16, jnp.float32
 
@@ -204,63 +226,81 @@
     rate_one = learn_rate / (1.0 - beta_one**ADAM_STEP)
     over_two = 1.0 / (1.0 - beta_two**ADAM_STEP)
 
-    def update(k):
+    wide = 4 if half % 4 == 0 else 1
+
+    def update(k, start, count):
         c = flip(z, k, shards)
 
-        def row(r, carry):
-            clipped = landed[c, r].astype(f32) * scale
-            new_first = beta_one * first[r, c] + (1.0 - beta_one) * clipped
-            new_second = beta_two * second[r, c] + (1.0 - beta_two) * clipped * clipped
-            below = jnp.sqrt(new_second * over_two) + adam_eps
-            new_master = master[r, c] - new_first * rate_one / below
-            master[r, c] = new_master
-            first[r, c] = new_first
-            second[r, c] = new_second
-            if k:
-                landed[c, r] = new_master.astype(bf16)
-            else:
-                out[g, z, r] = new_master.astype(bf16)
+        def some(i, carry):
+            for j in range(wide):
+                r = start + i * wide + j
+                clipped = landed[c, r].astype(f32) * scale
+                new_first = beta_one * first[r, c] + (1.0 - beta_one) * clipped
+                new_second = beta_two * second[r, c] + (1.0 - beta_two) * clipped * clipped
+                below = jnp.sqrt(new_second * over_two) + adam_eps
+                new_master = master[r, c] - new_first * rate_one / below
+                master[r, c] = new_master
+                first[r, c] = new_first
+                second[r, c] = new_second
+                if k:
+                    landed[c, r] = new_master.astype(bf16)
+                else:
+                    out[g, z, r] = new_master.astype(bf16)
             return carry
 
-        lax.fori_loop(0, rows, row, 0)
+        lax.fori_loop(0, count // wide, some, 0)
 
     def spread(k):
         return remote(landed.at[flip(z, k, shards)], out.at[g, z], z_send.at[k], z_recv.at[k],
                       (g, flip(z, k, shards)))
 
-    def first_hop(k, send, recv, to):
-        ref = out.at[g, flip(z, k, shards)]
-        return remote(ref, ref, send.at[k], recv.at[k], (to, z))
-
-    def second_hop(k, origin, start, send, recv, to):
-        ref = out.at[origin, flip(z, k, shards), pl.ds(start, half)]
-        return remote(ref, ref, send.at[k], recv.at[k], (to, z))
+    def arrival(k):
+        mask, q = partner(z, k, shards)
+        return remote(landed.at[q], out.at[g, z], z_send.at[mask], z_recv.at[mask], (g, q))
+
+    def hop(k, a, h):
+        ref = out.at[g, partner(z, k, shards)[1], pl.ds(h * half, half)]
+        held = late_y if a else late_x
+        target = held.at[late.index(k)] if k in late and a == h else ref
+        send, recv = (y_send, y_recv) if a else (x_send, x_recv)
+        return remote(ref, target, send.at[k, h], recv.at[k, h], (gy if a else gx, z))
+
+    def turn(k, a):
+        ref = out.at[gy if a else gx, partner(z, k, shards)[1], pl.ds(a * half, half)]
+        send, recv = (v_send, v_recv) if a else (u_send, u_recv)
+        return remote(ref, ref, send.at[k], recv.at[k], (gx if a else gy, z))
 
     def hops(k):
-        return (first_hop(k, x_send, x_recv, gx), first_hop(k, y_send, y_recv, gy))
-
-    def turns(k):
-        return (second_hop(k, gx, 0, u_send, u_recv, gy), second_hop(k, gy, half, v_send, v_recv, gx))
+        return [hop(k, a, h) for a, h in ((0, 0), (1, 1), (0, 1), (1, 0))]
+
+    def advance(k):
+        arrival(k).wait_recv()
+        for copy in hops(k):
+            copy.start()
+
+    def relay(k):
+        if k not in late:
+            for a in (0, 1):
+                hop(k, a, a).wait_recv()
+                turn(k, a).start()
 
     for state in states:
         state.wait()
-    update(0)
-    for hop in hops(0):
-        hop.start()
-    for k in range(1, shards):
+    for h in (0, 1):
+        update(0, h * half, half)
+        for a in (0, 1):
+            hop(0, a, h).start()
+    for i, k in enumerate(made):
         onward(k).wait_recv()
-        update(k)
+        update(k, 0, rows)
         spread(k).start()
-    lag = 1
-    for s in range(1, shards + lag):
+        if i == min(3, shards - 2):
+            advance(used[1])
+    relay(used[0])
+    for s in range(2, shards + 1):
         if s < shards:
-            spread(s).wait_recv()
-            for hop in hops(s):
-                hop.start()
-        if s >= lag:
-            for hop, turn in zip(hops(s - lag), turns(s - lag)):
-                hop.wait_recv()
-                turn.start()
+            advance(used[s])
+        relay(used[s - 1])
     for k in range(1, shards):
         tell_zero(k).wait_send()
         onward(k).wait_send()
@@ -271,10 +311,33 @@
         for h in (0, 1):
             for d in (0, 1):
                 raw(k, h, d).wait_send()
-        for hop in hops(k):
-            hop.wait_send()
-        for turn in turns(k):
-            turn.wait()
+        for a in (0, 1):
+            for h in (0, 1):
+                hop(k, a, h).wait_send()
+                if a != h or k in late:
+                    hop(k, a, h).wait_recv()
+            if k not in late:
+                turn(k, a).wait()
+
+
+def patch_kernel(groups, shards, tails, weights, late_x, late_y, came_x, came_y, out, sem):
+    del weights
+    g, z = lax.axis_index("grp"), lax.axis_index("zero")
+    gx, gy, diagonal = flip(g, 1, groups), flip(g, 2, groups), flip(g, 3, groups)
+    half = late_x.shape[1]
+    used, _ = orders(shards)
+    moves = []
+    for i, (source, origin, h) in enumerate(
+        ((late_x, gx, 0), (late_y, gy, 1), (came_x, diagonal, 0), (came_y, diagonal, 1))
+    ):
+        for t in range(tails):
+            q = partner(z, used[shards - tails + t], shards)[1]
+            moves.append(pltpu.make_async_copy(
+                source.at[t], out.at[origin, q, pl.ds(h * half, half)], sem.at[i, t]))
+    for move in moves:
+        move.start()
+    for move in moves:
+        move.wait()
 
 
 def store_kernel(pieces, *refs):
@@ -319,12 +382,18 @@
 
     block = (shards, rows, deep, LANES)
     state = (rows, shards, deep, LANES)
+    tails = min(3, shards - 1)
+    late = (tails, rows // 2, deep, LANES)
     grant = 4 * shards * rows * deep * LANES + 192 * 1024
     results = pl.pallas_call(
-        functools.partial(step_kernel, groups, shards),
-        out_shape=(*[pltpu.VMEM(state, f32)] * 3, pltpu.VMEM((groups,) + block, bf16)),
+        functools.partial(step_kernel, groups, shards, tails),
+        out_shape=(
+            *[pltpu.VMEM(state, f32)] * 3,
+            pltpu.VMEM((groups,) + block, bf16),
+            *[jax.ShapeDtypeStruct(late, bf16)] * 2,
+        ),
         in_specs=[pl.BlockSpec(memory_space=pltpu.SMEM)] + [any_space] * 4,
-        out_specs=(vmem,) * 4,
+        out_specs=(vmem,) * 4 + (any_space,) * 2,
         scratch_shapes=[
             *[pltpu.VMEM(block, bf16)] * 2,
             pltpu.VMEM((shards, 8, LANES), f32),
@@ -334,7 +403,9 @@
             *[dma((shards,))] * 4,
             *[dma((groups,))] * 2,
             dma((3,)),
-            *[dma((shards,))] * 10,
+            *[dma((shards,))] * 2,
+            *[dma((shards, 2))] * 4,
+            *[dma((shards,))] * 4,
         ],
         compiler_params=pltpu.CompilerParams(
             collective_id=0, has_side_effects=True, vmem_limit_bytes=grant
@@ -342,7 +413,9 @@
     )(max_norm, grad, master, first, second)
 
     pieces = 4
-    *states, gathered = results
+    *states, gathered, late_x, late_y = results
+    came_x = lax.ppermute(late_x, "grp", [(i, i ^ 2) for i in range(groups)])
+    came_y = lax.ppermute(late_y, "grp", [(i, i ^ 1) for i in range(groups)])
     new_master, new_first, new_second = pl.pallas_call(
         functools.partial(store_kernel, pieces),
         out_shape=(
@@ -352,7 +425,26 @@
         out_specs=(any_space,) * 3,
         scratch_shapes=[dma((3, pieces))],
         compiler_params=pltpu.CompilerParams(vmem_limit_bytes=grant),
+        cost_estimate=pl.CostEstimate(flops=0, bytes_accessed=8 * 3 * master.size, transcendentals=0),
     )(*states)
+    gathered = pl.pallas_call(
+        functools.partial(store_kernel, groups),
+        out_shape=jax.ShapeDtypeStruct((groups,) + block, bf16),
+        in_specs=[any_space],
+        out_specs=any_space,
+        scratch_shapes=[dma((1, groups))],
+        compiler_params=pltpu.CompilerParams(vmem_limit_bytes=grant),
+        cost_estimate=pl.CostEstimate(flops=0, bytes_accessed=4 * gathered.size, transcendentals=0),
+    )(gathered)
+    gathered = pl.pallas_call(
+        functools.partial(patch_kernel, groups, shards, tails),
+        out_shape=jax.ShapeDtypeStruct((groups,) + block, bf16),
+        in_specs=[any_space] * 5,
+        out_specs=any_space,
+        input_output_aliases={0: 0},
+        scratch_shapes=[dma((4, tails))],
+        compiler_params=pltpu.CompilerParams(vmem_limit_bytes=grant),
+    )(gathered, *[pltpu.with_memory_space_constraint(x, pltpu.VMEM) for x in (late_x, late_y, came_x, came_y)])
 
     def unflat(x, shape):
         x = x.reshape(shape[0], -1, 2, LANES)

time: 350 us -> 329 us (0.940)
  Pallas kernels: 342 us -> 322 us
  local copies, waits for them, and re-layouts: 6.85 us -> 0.01 us
  waiting for transfers between devices: 0 us -> 4.03 us
    pallas_call x1 -> x3, Pallas kernels: 332 us -> 312 us  [the longest x1 304 us: flat_body(): pl.pallas_call(functools.partial(step_kernel, groups, shards, tails), out...]
    unnamed x1 -> x4, local copies, waits for them, and re-layouts: 6.85 us -> 0.01 us
    ppermute x0 -> x2, waiting for transfers between devices: none -> 4.03 us  [the longest x1 3.76 us: flat_body(): came_x = lax.ppermute(late_x, 'grp', [(i, i ^ 2) for i in range(groups)])]
  transfers between devices with their start and end apart: 0 -> 2, of which waited for: 0 -> 2; matrix products, arithmetic and copies ran while one was open for 0% -> 0% of each run, Pallas kernels for 0% -> 5%
where the time goes in v2:
time: 329 us
  Pallas kernels  322 us (98%)
  waiting for transfers between devices  4.03 us (1%)
    pallas_call x1, Pallas kernels, flat_body(): pl.pallas_call(functools.partial(step_kernel, groups, shards, tails), out...  304 us
    pallas_call x1, Pallas kernels, flat_body(): pl.pallas_call(functools.partial(store_kernel, pieces), out_shape=(*[jax....  9.45 us
    pallas_call x1, Pallas kernels, flat_body(): pl.pallas_call(functools.partial(store_kernel, groups), out_shape=jax.Sha...  6.61 us
  transfers between devices with their start and end apart: 2, of which 2 were waited for; matrix products, arithmetic and copies ran while one was open for 0% of the time, Pallas kernels for 5%

profile of v2, /device:TPU:0, one launch (start us, length us, event | category | flops | bytes accessed | tf_op | source)
XLA Modules:
  0.0 329.0 jit_solution(8913198053415639496)
XLA Ops:
  1.3 303.6 %shard_map.84 = (f32[96,8,24,128]{3,2,1,0:T(8,128)S(1)}, f32[96,8,24,128]{3,2,1,0:T(8,128)S(1)}, f32[96,8,24,128]{3,2,1,0:T(8,128)S(1)}, bf16[4,8,96,24,128]{4,3...) custom-call(f32[1]{0:T(128)S(6)} %copy.11.limit, ...), custom_call_target="tpu_custom_call" | custom-call | tf_op jit(solution)/shard_map/pallas_call | solution.py:388
  304.9 0.2 collective-permute-start
  305.1 1.9 collective-permute-start.1
  307.0 6.6 %shard_map.86.weights = bf16[4,8,96,24,128]{4,3,2,1,0:T(8,128)(2,1)} custom-call(bf16[4,8,96,24,128]{4,3,2,1,0:T(8,128)(2,1)S(1)} %get-tuple-element.19.refs_0_), custom_call_target="tpu_custom_call" | custom-call | bytes 37748736 | tf_op jit(solution)/shard_map/pallas_call | solution.py:430
  313.6 0.0 copy-start
  313.6 0.0 copy-start.1
  313.6 9.5 %shard_map.85 = (f32[96,8,24,128]{3,2,1,0:T(8,128)}, f32[96,8,24,128]{3,2,1,0:T(8,128)}, f32[96,8,24,128]{3,2,1,0:T(8,128)}) custom-call(f32[96,8,24,128]{3,2,1,0:T(8,128)S(1)} %get-tuple-element.13.refs_0_, f32[96,8,24,128]{3,2,1,0:T(8,128)S(1)} %get-tuple-element.14.refs_1_, f32[96,8,24,128]{3,2,1,0:T(8,128)S(1)} %get-tuple-element.15.refs_2_), custom_call_target="tpu_custom_call" | custom-call | bytes 56623104 | tf_op jit(solution)/shard_map/pallas_call | solution.py:419
  323.1 3.8 %collective-permute-done.came_x = bf16[3,48,24,128]{3,2,1,0:T(8,128)(2,1)S(1)} collective-permute-done((bf16[3,48,24,128]{3,2,1,0:T(8,128)(2,1)}, bf16[3,48,24,128]{3,2,1,0:T(8,128)(2,1)S(1)}, u32[]{:S(2)}, u32[]{:S(2)}) %collective-permute-start) | collective-permute-done | bytes 884768 | tf_op jit(solution)/shard_map/ppermute | solution.py:417
  326.8 0.3 collective-permute-done.1.came_y
  327.1 0.0 copy-done
  327.1 0.0 copy-done.1
  327.1 1.9 shard_map.87
Async XLA Ops:
  304.9 21.9 %collective-permute-start = (bf16[3,48,24,128]{3,2,1,0:T(8,128)(2,1)}, bf16[3,48,24,128]{3,2,1,0:T(8,128)(2,1)S(1)}, u32[]{:S(2)}, u32[]{:S(2)}) collective-permute-start(bf16[3,48,24,128]{3,2,1,0:T(8,128)(2,1)} %get-tuple-element.20.late_x), channel_id=1, source_target_pairs={{0,16},{8,24},{16,0},{24,8},{1,17},{9,25},{17,1},{25,9},{2,18},{10... | collective-permute-start | bytes 2654216 | tf_op jit(solution)/shard_map/ppermute | solution.py:417
  305.1 22.0 %collective-permute-start.1 = (bf16[3,48,24,128]{3,2,1,0:T(8,128)(2,1)}, bf16[3,48,24,128]{3,2,1,0:T(8,128)(2,1)S(1)}, u32[]{:S(2)}, u32[]{:S(2)}) collective-permute-start(bf16[3,48,24,128]{3,2,1,0:T(8,128)(2,1)} %get-tuple-element.21.late_y), channel_id=1, source_target_pairs={{0,8},{8,0},{16,24},{24,16},{1,9},{9,1},{17,25},{25,17},{2,10},{10... | collective-permute-start | bytes 2654216 | tf_op jit(solution)/shard_map/ppermute | solution.py:418
  313.6 13.5 %copy-start = (bf16[3,48,24,128]{3,2,1,0:T(8,128)(2,1)S(1)}, bf16[3,48,24,128]{3,2,1,0:T(8,128)(2,1)}, u32[]{:S(2)}) copy-start(bf16[3,48,24,128]{3,2,1,0:T(8,128)(2,1)} %get-tuple-element.20.late_x) | copy-start | bytes 2654212
  313.6 13.5 %copy-start.1 = (bf16[3,48,24,128]{3,2,1,0:T(8,128)(2,1)S(1)}, bf16[3,48,24,128]{3,2,1,0:T(8,128)(2,1)}, u32[]{:S(2)}) copy-start(bf16[3,48,24,128]{3,2,1,0:T(8,128)(2,1)} %get-tuple-element.21.late_y) | copy-start | bytes 2654212

commit v3 on v2

--- a/solution.py
+++ b/solution.py
@@ -107,8 +107,8 @@
 
 def step_kernel(groups, shards, tails, limit, grad, master_in, first_in, second_in, master, first, second, out,
                 late_x, late_y, sums, landed, zone, gone, f_send, f_recv, load_sem, p_send, p_recv, s_send, s_recv,
-                nz_send, nz_recv, ng_send, ng_recv, state_sem, z_send, z_recv, x_send, x_recv, y_send, y_recv,
-                u_send, u_recv, v_send, v_recv):
+                nz_send, nz_recv, ng_send, ng_recv, state_sem, ready_sem, z_send, z_recv, x_send, x_recv, y_send, y_recv,
+                u_send, u_recv, v_send, v_recv, l_send, l_recv):
     g, z = lax.axis_index("grp"), lax.axis_index("zero")
     gx, gy, diagonal = flip(g, 1, groups), flip(g, 2, groups), flip(g, 3, groups)
     first_to, second_to = (gx, gy), (gy, gx)
@@ -119,13 +119,20 @@
     late = used[shards - tails:]
     near, far, got, pairs = (out.at[i] for i in range(4))
     bf16, f32 = jnp.bfloat16, jnp.float32
+    wide = 4
+    first_rows = half // 4
 
     def part(ref, k, h):
         return ref.at[k, pl.ds(h * half, half)]
 
+    def ready(h):
+        return pltpu.make_async_copy(grad.at[diagonal, flip(z, order[0], shards), h], part(landed, z, h),
+                                     ready_sem.at[h])
+
     def raw(k, h, d):
         block = diagonal if d else first_to[h]
-        return remote(grad.at[block, flip(z, k, shards), h], part(far if d else near, k, h),
+        source = part(landed, z, h) if d and k == order[0] else grad.at[block, flip(z, k, shards), h]
+        return remote(source, part(far if d else near, k, h),
                       f_send.at[k, h, d], f_recv.at[k, h, d], (first_to[h], z))
 
     def pair(k, h):
@@ -144,10 +151,14 @@
         for i, (src, dst) in enumerate(((master_in, master), (first_in, first), (second_in, second)))
     ]
 
+    for h in (0, 1):
+        ready(h).start()
     greet(groups, shards, g, z)
     ahead = 2
     for k in order[:ahead]:
         for h in (0, 1):
+            if k == order[0]:
+                ready(h).wait()
             raw(k, h, 1).start()
     for k in order:
         for d in (1, 0):
@@ -163,13 +174,14 @@
                 load(k, h, 1).wait()
                 raw(k, h, 1).wait_recv()
 
-                def join(r, carry, k=k, h=h):
-                    row = h * half + r
-                    both = pairs[k, row].astype(f32) + far[k, row].astype(f32)
-                    pairs[k, row] = both.astype(bf16)
+                def join(i, carry, k=k, h=h):
+                    for j in range(wide):
+                        row = h * half + i * wide + j
+                        both = pairs[k, row].astype(f32) + far[k, row].astype(f32)
+                        pairs[k, row] = both.astype(bf16)
                     return carry
 
-                lax.fori_loop(0, half, join, 0)
+                lax.fori_loop(0, half // wide, join, 0)
                 pair(k, h).start()
             for h in (0, 1):
                 raw(k, h, 0).start()
@@ -179,21 +191,28 @@
         if i >= 1:
             k = order[i - 1]
             for h in (0, 1):
+                if k == 0:
+                    raw(order[0], h, 1).wait_send()
                 load(k, h, 0).wait()
                 raw(k, h, 0).wait_recv()
                 pair(k, h).wait_recv()
 
-                def add(r, acc, k=k, h=h):
-                    row = h * half + r
-                    total = sums[k, row].astype(f32) + near[k, row].astype(f32)
-                    total = total + got[k, row].astype(f32)
-                    if k:
-                        sums[k, row] = total.astype(bf16)
-                    else:
-                        landed[z, row] = total.astype(bf16)
-                    return acc + total * total
-
-                square = lax.fori_loop(0, half, add, square)
+                def add(i, acc, k=k, h=h):
+                    parts = []
+                    for j in range(wide):
+                        row = h * half + i * wide + j
+                        total = sums[k, row].astype(f32) + near[k, row].astype(f32)
+                        total = total + got[k, row].astype(f32)
+                        if k:
+                            sums[k, row] = total.astype(bf16)
+                        else:
+                            landed[z, row] = total.astype(bf16)
+                        parts.append(total * total)
+                    while len(parts) > 1:
+                        parts = [sum(parts[i:i + 2]) for i in range(0, len(parts), 2)]
+                    return acc + parts[0]
+
+                square = lax.fori_loop(0, half // wide, add, square)
             if k:
                 onward(k).start()
 
@@ -226,8 +245,6 @@
     rate_one = learn_rate / (1.0 - beta_one**ADAM_STEP)
     over_two = 1.0 / (1.0 - beta_two**ADAM_STEP)
 
-    wide = 4 if half % 4 == 0 else 1
-
     def update(k, start, count):
         c = flip(z, k, shards)
 
@@ -259,12 +276,17 @@
         return remote(landed.at[q], out.at[g, z], z_send.at[mask], z_recv.at[mask], (g, q))
 
     def hop(k, a, h):
-        ref = out.at[g, partner(z, k, shards)[1], pl.ds(h * half, half)]
+        skip = first_rows if k == 0 and h == 0 else 0
+        ref = out.at[g, partner(z, k, shards)[1], pl.ds(h * half + skip, half - skip)]
         held = late_y if a else late_x
         target = held.at[late.index(k)] if k in late and a == h else ref
         send, recv = (y_send, y_recv) if a else (x_send, x_recv)
         return remote(ref, target, send.at[k, h], recv.at[k, h], (gy if a else gx, z))
 
+    def lead(a):
+        ref = out.at[g, z, pl.ds(0, first_rows)]
+        return remote(ref, ref, l_send.at[a], l_recv.at[a], (gy if a else gx, z))
+
     def turn(k, a):
         ref = out.at[gy if a else gx, partner(z, k, shards)[1], pl.ds(a * half, half)]
         send, recv = (v_send, v_recv) if a else (u_send, u_recv)
@@ -278,62 +300,101 @@
         for copy in hops(k):
             copy.start()
 
+    def finish(k):
+        if k:
+            spread(k).wait_send()
+        for a in (0, 1):
+            for h in (0, 1):
+                hop(k, a, h).wait_send()
+                if a != h or k in late:
+                    hop(k, a, h).wait_recv()
+            if k == 0:
+                lead(a).wait_send()
+                if a:
+                    lead(a).wait_recv()
+            if k not in late:
+                turn(k, a).wait()
+
     def relay(k):
         if k not in late:
             for a in (0, 1):
                 hop(k, a, a).wait_recv()
+                if k == 0 and a == 0:
+                    lead(a).wait_recv()
                 turn(k, a).start()
 
     for state in states:
         state.wait()
-    for h in (0, 1):
-        update(0, h * half, half)
+    update(0, 0, first_rows)
+    for a in (0, 1):
+        lead(a).start()
+    for h, skip in ((0, first_rows), (1, 0)):
+        update(0, h * half + skip, half - skip)
         for a in (0, 1):
             hop(0, a, h).start()
     for i, k in enumerate(made):
         onward(k).wait_recv()
         update(k, 0, rows)
         spread(k).start()
-        if i == min(3, shards - 2):
+        if i == 3:
             advance(used[1])
+    for k in range(1, shards):
+        tell_zero(k).wait_send()
+        onward(k).wait_send()
+    for j in range(1, groups):
+        tell_group(j).wait_send()
+    for k in order:
+        for h in (0, 1):
+            for d in (0, 1):
+                if d == 0 or k != order[0]:
+                    raw(k, h, d).wait_send()
     relay(used[0])
     for s in range(2, shards + 1):
         if s < shards:
             advance(used[s])
         relay(used[s - 1])
-    for k in range(1, shards):
-        tell_zero(k).wait_send()
-        onward(k).wait_send()
-        spread(k).wait_send()
-    for j in range(1, groups):
-        tell_group(j).wait_send()
-    for k in order:
-        for h in (0, 1):
-            for d in (0, 1):
-                raw(k, h, d).wait_send()
-        for a in (0, 1):
-            for h in (0, 1):
-                hop(k, a, h).wait_send()
-                if a != h or k in late:
-                    hop(k, a, h).wait_recv()
-            if k not in late:
-                turn(k, a).wait()
-
-
-def patch_kernel(groups, shards, tails, weights, late_x, late_y, came_x, came_y, out, sem):
-    del weights
-    g, z = lax.axis_index("grp"), lax.axis_index("zero")
-    gx, gy, diagonal = flip(g, 1, groups), flip(g, 2, groups), flip(g, 3, groups)
-    half = late_x.shape[1]
+        if s >= 4:
+            finish(used[s - 4])
+    for k in used[shards - 3:]:
+        finish(k)
+
+
+def late_moves(groups, shards, tails, sources, origins, out, sem):
+    z = lax.axis_index("zero")
     used, _ = orders(shards)
+    half = out.shape[2] // 2
     moves = []
-    for i, (source, origin, h) in enumerate(
-        ((late_x, gx, 0), (late_y, gy, 1), (came_x, diagonal, 0), (came_y, diagonal, 1))
-    ):
+    for h in (0, 1):
         for t in range(tails):
             q = partner(z, used[shards - tails + t], shards)[1]
             moves.append(pltpu.make_async_copy(
-                source.at[t], out.at[origin, q, pl.ds(h * half, half)], sem.at[i, t]))
+                sources[h].at[t], out.at[origins[h], q, pl.ds(h * half, half)], sem.at[h, t]))
+    return moves
+
+
+def weight_kernel(groups, shards, tails, gathered, late_x, late_y, out, hold_x, hold_y, load_sem, sem, late_sem):
+    g = lax.axis_index("grp")
+    origins = (flip(g, 1, groups), flip(g, 2, groups))
+    loads = [
+        pltpu.make_async_copy(late_x, hold_x, load_sem.at[0]),
+        pltpu.make_async_copy(late_y, hold_y, load_sem.at[1]),
+    ]
+    copies = [pltpu.make_async_copy(gathered.at[i], out.at[i], sem.at[i]) for i in range(groups)]
+    moves = late_moves(groups, shards, tails, (hold_x, hold_y), origins, out, late_sem)
+    for copy in loads + copies:
+        copy.start()
+    for copy in loads + copies:
+        copy.wait()
+    for copy in moves:
+        copy.start()
+    for copy in moves:
+        copy.wait()
+
+
+def patch_kernel(groups, shards, tails, weights, came_x, came_y, out, sem):
+    del weights
+    diagonal = flip(lax.axis_index("grp"), 3, groups)
+    moves = late_moves(groups, shards, tails, (came_x, came_y), (diagonal, diagonal), out, sem)
     for move in moves:
         move.start()
     for move in moves:
@@ -382,7 +443,7 @@
 
     block = (shards, rows, deep, LANES)
     state = (rows, shards, deep, LANES)
-    tails = min(3, shards - 1)
+    tails = 3
     late = (tails, rows // 2, deep, LANES)
     grant = 4 * shards * rows * deep * LANES + 192 * 1024
     results = pl.pallas_call(
@@ -403,9 +464,11 @@
             *[dma((shards,))] * 4,
             *[dma((groups,))] * 2,
             dma((3,)),
+            dma((2,)),
             *[dma((shards,))] * 2,
             *[dma((shards, 2))] * 4,
             *[dma((shards,))] * 4,
+            *[dma((2,))] * 2,
         ],
         compiler_params=pltpu.CompilerParams(
             collective_id=0, has_side_effects=True, vmem_limit_bytes=grant
@@ -428,23 +491,23 @@
         cost_estimate=pl.CostEstimate(flops=0, bytes_accessed=8 * 3 * master.size, transcendentals=0),
     )(*states)
     gathered = pl.pallas_call(
-        functools.partial(store_kernel, groups),
+        functools.partial(weight_kernel, groups, shards, tails),
         out_shape=jax.ShapeDtypeStruct((groups,) + block, bf16),
-        in_specs=[any_space],
+        in_specs=[any_space] * 3,
         out_specs=any_space,
-        scratch_shapes=[dma((1, groups))],
+        scratch_shapes=[*[pltpu.VMEM(late, bf16)] * 2, dma((2,)), dma((groups,)), dma((2, tails))],
         compiler_params=pltpu.CompilerParams(vmem_limit_bytes=grant),
         cost_estimate=pl.CostEstimate(flops=0, bytes_accessed=4 * gathered.size, transcendentals=0),
-    )(gathered)
+    )(gathered, *[pltpu.with_memory_space_constraint(x, pltpu.HBM) for x in (late_x, late_y)])
     gathered = pl.pallas_call(
         functools.partial(patch_kernel, groups, shards, tails),
         out_shape=jax.ShapeDtypeStruct((groups,) + block, bf16),
-        in_specs=[any_space] * 5,
+        in_specs=[any_space] * 3,
         out_specs=any_space,
         input_output_aliases={0: 0},
-        scratch_shapes=[dma((4, tails))],
+        scratch_shapes=[dma((2, tails))],
         compiler_params=pltpu.CompilerParams(vmem_limit_bytes=grant),
-    )(gathered, *[pltpu.with_memory_space_constraint(x, pltpu.VMEM) for x in (late_x, late_y, came_x, came_y)])
+    )(gathered, *[pltpu.with_memory_space_constraint(x, pltpu.VMEM) for x in (came_x, came_y)])
 
     def unflat(x, shape):
         x = x.reshape(shape[0], -1, 2, LANES)
@@ -465,9 +528,9 @@
     rows = master_weights.shape[0]
     width = replica_grads.shape[3]
     deep = 2 * width // LANES
-    power = shards > 1 and shards & (shards - 1) == 0
+    power = shards >= 8 and shards & (shards - 1) == 0
     fits = shards * rows * deep * LANES * (2 * groups + 12 + 4) < 63 * 1024 * 1024
-    whole = width % LANES == 0 and deep % 8 == 0 and rows % 2 == 0
+    whole = width % LANES == 0 and deep % 8 == 0 and rows % 32 == 0
     run = flat_body if groups == 4 and power and fits and whole else plain_body
     return run(replica_grads, master_weights, first_moment, second_moment, max_norm)
 

time: 329 us -> 327 us (level)
  no operation moved by 1% of the time
where the time goes in v3:
time: 327 us
  Pallas kernels  320 us (98%)
  waiting for transfers between devices  3.45 us (1%)
    pallas_call x1, Pallas kernels, flat_body(): pl.pallas_call(functools.partial(step_kernel, groups, shards, tails), out...  302 us
    pallas_call x1, Pallas kernels, flat_body(): pl.pallas_call(functools.partial(store_kernel, pieces), out_shape=(*[jax....  9.45 us
    pallas_call x1, Pallas kernels, flat_body(): pl.pallas_call(functools.partial(weight_kernel, groups, shards, tails), o...  7.88 us
  transfers between devices with their start and end apart: 2, of which 2 were waited for; matrix products, arithmetic and copies ran while one was open for 0% of the time, Pallas kernels for 5%

profile of v3, /device:TPU:0, one launch (start us, length us, event | category | flops | bytes accessed | tf_op | source)
XLA Modules:
  0.0 327.3 jit_solution(5914308994076747883)
XLA Ops:
  1.3 301.9 %shard_map.84 = (f32[96,8,24,128]{3,2,1,0:T(8,128)S(1)}, f32[96,8,24,128]{3,2,1,0:T(8,128)S(1)}, f32[96,8,24,128]{3,2,1,0:T(8,128)S(1)}, bf16[4,8,96,24,128]{4,3...) custom-call(f32[1]{0:T(128)S(6)} %copy.11.limit, ...), custom_call_target="tpu_custom_call" | custom-call | tf_op jit(solution)/shard_map/pallas_call | solution.py:449
  303.2 0.4 collective-permute-start
  303.6 1.7 collective-permute-start.1
  305.2 7.9 %shard_map.86.weights = bf16[4,8,96,24,128]{4,3,2,1,0:T(8,128)(2,1)} custom-call(bf16[4,8,96,24,128]{4,3,2,1,0:T(8,128)(2,1)S(1)} %get-tuple-element.19.gathered, bf16[3,48,24,128]{3,2,1,0:T(8,128)(2,1)} %get-tuple-element.20.late_x, bf16[3,48,24,128]{3,2,1,0:T(8,128)(2,1)} %get-tuple-element.21.late_y), custom_call_target="tpu_custom_call" | custom-call | bytes 37748736 | tf_op jit(solution)/shard_map/pallas_call | solution.py:493
  313.1 9.5 %shard_map.85 = (f32[96,8,24,128]{3,2,1,0:T(8,128)}, f32[96,8,24,128]{3,2,1,0:T(8,128)}, f32[96,8,24,128]{3,2,1,0:T(8,128)}) custom-call(f32[96,8,24,128]{3,2,1,0:T(8,128)S(1)} %get-tuple-element.13.refs_0_, f32[96,8,24,128]{3,2,1,0:T(8,128)S(1)} %get-tuple-element.14.refs_1_, f32[96,8,24,128]{3,2,1,0:T(8,128)S(1)} %get-tuple-element.15.refs_2_), custom_call_target="tpu_custom_call" | custom-call | bytes 56623104 | tf_op jit(solution)/shard_map/pallas_call | solution.py:482
  322.6 3.2 collective-permute-done.came_x
  325.8 0.3 collective-permute-done.1.came_y
  326.0 1.2 shard_map.87
Async XLA Ops:
  303.2 22.6 %collective-permute-start = (bf16[3,48,24,128]{3,2,1,0:T(8,128)(2,1)}, bf16[3,48,24,128]{3,2,1,0:T(8,128)(2,1)S(1)}, u32[]{:S(2)}, u32[]{:S(2)}) collective-permute-start(bf16[3,48,24,128]{3,2,1,0:T(8,128)(2,1)} %get-tuple-element.20.late_x), channel_id=1, source_target_pairs={{0,16},{8,24},{16,0},{24,8},{1,17},{9,25},{17,1},{25,9},{2,18},{10... | collective-permute-start | bytes 2654216 | tf_op jit(solution)/shard_map/ppermute | solution.py:480
  303.6 22.5 %collective-permute-start.1 = (bf16[3,48,24,128]{3,2,1,0:T(8,128)(2,1)}, bf16[3,48,24,128]{3,2,1,0:T(8,128)(2,1)S(1)}, u32[]{:S(2)}, u32[]{:S(2)}) collective-permute-start(bf16[3,48,24,128]{3,2,1,0:T(8,128)(2,1)} %get-tuple-element.21.late_y), channel_id=1, source_target_pairs={{0,8},{8,0},{16,24},{24,16},{1,9},{9,1},{17,25},{25,17},{2,10},{10... | collective-permute-start | bytes 2654216 | tf_op jit(solution)/shard_map/ppermute | solution.py:481

commit v4 on v3

--- a/solution.py
+++ b/solution.py
@@ -171,6 +171,8 @@
         if i < shards:
             k = order[i]
             for h in (0, 1):
+                raw(k, h, 0).start()
+            for h in (0, 1):
                 load(k, h, 1).wait()
                 raw(k, h, 1).wait_recv()
 
@@ -183,8 +185,6 @@
 
                 lax.fori_loop(0, half // wide, join, 0)
                 pair(k, h).start()
-            for h in (0, 1):
-                raw(k, h, 0).start()
             if i + ahead < shards:
                 for h in (0, 1):
                     raw(order[i + ahead], h, 1).start()

time: 327 us -> 327 us (level)
  no operation moved by 1% of the time
where the time goes in v4:
time: 327 us
  Pallas kernels  320 us (98%)
  waiting for transfers between devices  3.43 us (1%)
    pallas_call x1, Pallas kernels, flat_body(): pl.pallas_call(functools.partial(step_kernel, groups, shards, tails), out...  302 us
    pallas_call x1, Pallas kernels, flat_body(): pl.pallas_call(functools.partial(store_kernel, pieces), out_shape=(*[jax....  9.45 us
    pallas_call x1, Pallas kernels, flat_body(): pl.pallas_call(functools.partial(weight_kernel, groups, shards, tails), o...  7.88 us
  transfers between devices with their start and end apart: 2, of which 2 were waited for; matrix products, arithmetic and copies ran while one was open for 0% of the time, Pallas kernels for 5%

profile of v4, /device:TPU:0, one launch (start us, length us, event | category | flops | bytes accessed | tf_op | source)
XLA Modules:
  0.0 327.3 jit_solution(9947096566780281416)
XLA Ops:
  1.3 301.9 %shard_map.84 = (f32[96,8,24,128]{3,2,1,0:T(8,128)S(1)}, f32[96,8,24,128]{3,2,1,0:T(8,128)S(1)}, f32[96,8,24,128]{3,2,1,0:T(8,128)S(1)}, bf16[4,8,96,24,128]{4,3...) custom-call(f32[1]{0:T(128)S(6)} %copy.11.limit, ...), custom_call_target="tpu_custom_call" | custom-call | tf_op jit(solution)/shard_map/pallas_call | solution.py:449
  303.2 0.4 collective-permute-start
  303.6 1.7 collective-permute-start.1
  305.3 7.9 %shard_map.86.weights = bf16[4,8,96,24,128]{4,3,2,1,0:T(8,128)(2,1)} custom-call(bf16[4,8,96,24,128]{4,3,2,1,0:T(8,128)(2,1)S(1)} %get-tuple-element.19.gathered, bf16[3,48,24,128]{3,2,1,0:T(8,128)(2,1)} %get-tuple-element.20.late_x, bf16[3,48,24,128]{3,2,1,0:T(8,128)(2,1)} %get-tuple-element.21.late_y), custom_call_target="tpu_custom_call" | custom-call | bytes 37748736 | tf_op jit(solution)/shard_map/pallas_call | solution.py:493
  313.1 9.5 %shard_map.85 = (f32[96,8,24,128]{3,2,1,0:T(8,128)}, f32[96,8,24,128]{3,2,1,0:T(8,128)}, f32[96,8,24,128]{3,2,1,0:T(8,128)}) custom-call(f32[96,8,24,128]{3,2,1,0:T(8,128)S(1)} %get-tuple-element.13.refs_0_, f32[96,8,24,128]{3,2,1,0:T(8,128)S(1)} %get-tuple-element.14.refs_1_, f32[96,8,24,128]{3,2,1,0:T(8,128)S(1)} %get-tuple-element.15.refs_2_), custom_call_target="tpu_custom_call" | custom-call | bytes 56623104 | tf_op jit(solution)/shard_map/pallas_call | solution.py:482
  322.6 3.1 collective-permute-done.came_x
  325.8 0.3 collective-permute-done.1.came_y
  326.0 1.2 shard_map.87
Async XLA Ops:
  303.2 22.6 %collective-permute-start = (bf16[3,48,24,128]{3,2,1,0:T(8,128)(2,1)}, bf16[3,48,24,128]{3,2,1,0:T(8,128)(2,1)S(1)}, u32[]{:S(2)}, u32[]{:S(2)}) collective-permute-start(bf16[3,48,24,128]{3,2,1,0:T(8,128)(2,1)} %get-tuple-element.20.late_x), channel_id=1, source_target_pairs={{0,16},{8,24},{16,0},{24,8},{1,17},{9,25},{17,1},{25,9},{2,18},{10... | collective-permute-start | bytes 2654216 | tf_op jit(solution)/shard_map/ppermute | solution.py:480
  303.6 22.4 %collective-permute-start.1 = (bf16[3,48,24,128]{3,2,1,0:T(8,128)(2,1)}, bf16[3,48,24,128]{3,2,1,0:T(8,128)(2,1)S(1)}, u32[]{:S(2)}, u32[]{:S(2)}) collective-permute-start(bf16[3,48,24,128]{3,2,1,0:T(8,128)(2,1)} %get-tuple-element.21.late_y), channel_id=1, source_target_pairs={{0,8},{8,0},{16,24},{24,16},{1,9},{9,1},{17,25},{25,17},{2,10},{10... | collective-permute-start | bytes 2654216 | tf_op jit(solution)/shard_map/ppermute | solution.py:481
